TPU v7x, 32 devices: a whole 2x2x4 slice. The times are simulated.
32 devices in a mesh: tp: 4 (over z), dp: 8 (over y, x, core).
Axes of the slice: x: 2, y: 2, z: 4, core: 2. Of those that a mesh axis runs over, the one named last changes fastest.
Arguments:
- x_in: bfloat16 [4096, 2304], P('dp')
- w_gate: bfloat16 [2304, 9216], P('dp', 'tp')
- w_up: bfloat16 [2304, 9216], P('dp', 'tp')
- w_down: bfloat16 [9216, 2304], P('tp', 'dp')
- dy_in: bfloat16 [4096, 2304], P('dp')
Outputs:
- output 1: bfloat16 [4096, 2304], P('dp')
- output 2: bfloat16 [4096, 2304], P('dp')
- output 3: float32 [2304, 9216], P('dp', 'tp')
- output 4: float32 [2304, 9216], P('dp', 'tp')
- output 5: float32 [9216, 2304], P('tp', 'dp')
All inputs are finite; a program needn't handle non-finite values.
Results may differ from a plain program's by a relative error of at most 0.001.
Values are sent between devices in bfloat16 or wider.
A program may use at most 1 GiB of HBM per device.

v0:
```python
import functools
import math

import jax
import jax.numpy as jnp
from jax import lax
from jax.experimental import pallas as pl
from jax.experimental.pallas import tpu as pltpu
from jax.sharding import PartitionSpec as P

F32 = jnp.float32
BF16 = jnp.bfloat16
MESH = pl.DeviceIdType.MESH
SLOTS = 8
DEPTH = 13
KEEP = 16
LAG = 3
HOP = 2
LANES = 128
ONE = 1.0
BOTH = (0, 1)
ALL = (0, 1, 2)
EARLY = 4
MIDDLE = 8


def odd(n):
    return lax.rem(n, 2)


def halved(n):
    return lax.div(n, 2)


def dot_nn(a, b):
    return jnp.dot(a, b, preferred_element_type=F32)


def dot_nt(a, b):
    return lax.dot_general(a, b, (((1,), (1,)), ((), ())), preferred_element_type=F32)


def dot_tn(a, b):
    return lax.dot_general(a, b, (((0,), (0,)), ((), ())), preferred_element_type=F32)


def sigmoid(a):
    return ONE / (ONE + jnp.exp(-a))


def kernel(x_ref, dy_ref, wg_ref, wu_ref, wd_ref,
           yd_ref, acc_gu, acc_d, pbuf, yacc, w_gu, xb, dyb, xp, dyp,
           w_d, sb, xt, dyt, ab_all, g_s, h_all, rbuf, back,
           w_send, w_recv, wr_send, wr_recv, w_own, wp_send, wp_recv,
           own_send, own_recv, q_send, q_recv, rl_send, f_send, f_recv,
           y_send, y_recv, dx_send, dx_recv, credit, room,
           rs_send, rs_recv, ag_send, ag_recv, fin_own, ld, out_send, out_recv, h_send, h_recv, back_in):
    rows, model = x_ref.shape
    blk, width = wg_ref.shape
    half = width // 2
    third = width // 3
    half_cut = half // 2 // LANES * LANES
    low = pl.ds(0, half)
    whole = pl.ds(0, width)
    pair = 2 * blk
    hb = blk // 2
    tile = rows // 2
    piece = tile // 4
    parcel = 2 * piece
    win = acc_d.shape[0]
    line = model // 2
    units = line // LANES
    near_units = (pair - LANES // 2) // LANES if pair % LANES else pair // LANES
    rest_units = units - near_units
    steps = 4 * units
    part_rows = tile // 2
    total = 2 * steps
    group = min(32, tile)
    w_in = (wg_ref, wu_ref, wd_ref)
    cut = (half + 255) // 256 * 256
    pieces = ((0, cut), (cut, width))
    cut_ab = cut
    cut_g = half // 2 // 256 * 256
    tok = (x_ref, dy_ref)
    tok_b = (xb, dyb)
    tok_p = (xp, dyp)
    tok_t = (xt, dyt)

    t = lax.axis_index('tp')
    me = lax.axis_index('dp')
    cy = lax.div(me, 4)
    cx = lax.rem(halved(me), 2)
    far_y = 1 - cy
    far_x = 1 - cx
    j = odd(me)
    other_core = 1 - j
    partner = me + 1 - 2 * j
    chip = cy * 2 + cx

    def near(link, core):
        if link == 0:
            return cy * 4 + (far_x) * 2 + core
        return (far_y) * 4 + cx * 2 + core

    def far(core):
        return (far_y) * 4 + (far_x) * 2 + core

    def send(src, dst, s_sem, r_sem, dp=None, tp=None):
        where = {'dp': me if dp is None else dp, 'tp': t if tp is None else tp}
        return pltpu.make_async_remote_copy(src_ref=src, dst_ref=dst, send_sem=s_sem, recv_sem=r_sem,
                                            device_id=where, device_id_type=MESH)

    def wait(ref, sem):
        pltpu.make_async_copy(ref, ref, sem).wait()

    barrier = pltpu.get_barrier_semaphore()
    for peer in (partner, near(0, 0), near(0, 1), near(1, 0), near(1, 1)):
        pl.semaphore_signal(barrier, device_id={'dp': peer, 'tp': t}, device_id_type=MESH)

    @pl.when(t > 0)
    def _():
        pl.semaphore_signal(barrier, device_id={'dp': me, 'tp': t - 1}, device_id_type=MESH)

    @pl.when(t < 3)
    def _():
        pl.semaphore_signal(barrier, device_id={'dp': me, 'tp': t + 1}, device_id_type=MESH)

    pl.semaphore_wait(barrier, 5 + jnp.minimum(t, 1) + jnp.minimum(3 - t, 1))

    def w_rows(k, dev, part=None):
        if part is None:
            at = pl.ds(pl.multiple_of(dev * blk, 16), blk)
        else:
            at = pl.ds(pl.multiple_of(dev * blk + part * hb, 16), hb)
        if k == 2:
            return w_d.at[at, :]
        return w_gu.at[at, pl.ds(k * half, half)]

    def w_cols(core):
        return pl.ds(pl.multiple_of(core * half, LANES), half)

    def w_copy(k, link, part, core):
        return send(w_in[k].at[pl.ds(part * hb, hb), w_cols(core)], w_rows(k, me, part),
                    w_send.at[k, link, part, core], w_recv.at[k, link, part, j], dp=near(link, core))

    def w_own_copy(k):
        return pltpu.make_async_copy(w_in[k].at[:, w_cols(j)], w_rows(k, me), w_own.at[k])

    def w_partner_copy(k):
        return send(w_in[k].at[:, w_cols(other_core)], w_rows(k, me), wp_send.at[k], wp_recv.at[k], dp=partner)

    def w_start(k):
        for first in BOTH:
            for core in BOTH:
                w_copy(k, 0, 1 - first, core).start()
                w_copy(k, 1, first, core).start()
        w_own_copy(k).start()
        w_partner_copy(k).start()

    def w_relay_copy(k, link_out, core):
        part = 1 if link_out == 1 else 0
        ref = w_rows(k, near(1 - link_out, core), part)
        return send(ref, ref, wr_send.at[k, link_out, core], wr_recv.at[k, link_out, core], dp=near(link_out, j))

    def w_relay(k):
        for core in BOTH:
            wait(w_rows(k, near(0, core), 1), w_recv.at[k, 0, 1, core])
            w_relay_copy(k, 1, core).start()
            wait(w_rows(k, near(1, core), 0), w_recv.at[k, 1, 0, core])
            w_relay_copy(k, 0, core).start()

    def w_relayed(which):
        for k in which:
            for link in BOTH:
                for core in BOTH:
                    w_relay_copy(k, link, core).wait_send()

    def w_have(k, which):
        if which == 'chip':
            wait(w_rows(k, me), w_own.at[k])
            wait(w_rows(k, partner), wp_recv.at[k])
        for core in BOTH:
            if which == 'x':
                wait(w_rows(k, near(0, core), 0), w_recv.at[k, 0, 0, core])
            if which == 'y':
                wait(w_rows(k, near(1, core), 1), w_recv.at[k, 1, 1, core])
            if which == 'far':
                wait(w_rows(k, far(core), 0), wr_recv.at[k, 0, core])
                wait(w_rows(k, far(core), 1), wr_recv.at[k, 1, core])

    def slot_of(ten, q, link):
        return tok_b[ten].at[q, pl.ds(link * piece, piece), :]

    def q_copy(ten, q, link):
        b = lax.div(q, 4)
        sub = lax.rem(q, 4)
        first = 1 - b if link == 0 else b
        src = tok[ten].at[pl.ds(pl.multiple_of(first * tile + sub * piece, piece), piece), :]
        return send(src, slot_of(ten, q, link), q_send.at[q, link, ten], q_recv.at[q, link, ten], dp=near(link, j))

    def q_start(q):
        for ten in BOTH:
            for link in BOTH:
                q_copy(ten, q, link).start()

    def relay_copy(ten, sub, link_out):
        return send(slot_of(ten, sub, 1 - link_out), slot_of(ten, 8 + sub, link_out),
                    rl_send.at[sub, link_out, ten], q_recv.at[8 + sub, link_out, ten], dp=near(link_out, j))

    def tile_part(ten, q, core):
        return tok_t[ten].at[odd(q), pl.ds(pl.multiple_of(core * parcel, parcel), parcel), :]

    def forward_copy(ten, q):
        return send(tok_b[ten].at[q], tile_part(ten, q, j), f_send.at[q, ten], f_recv.at[q, ten], dp=partner)

    def own_copy(ten):
        return send(tok[ten], tok_p[ten], own_send.at[ten], own_recv.at[ten], dp=partner)

    def arrive(ten, q):
        with jax.named_scope('arrive'):
            for link in BOTH:
                wait(slot_of(ten, q, link), q_recv.at[q, link, ten])
            if ten == 0:
                pl.semaphore_wait(room.at[0])
            else:
                @pl.when(q < 11)
                def _():
                    pl.semaphore_wait(room.at[1])

            forward_copy(ten, q).start()
            pltpu.make_async_copy(tok_b[ten].at[q], tile_part(ten, q, j), ld.at[ten, odd(q)]).start()

        @pl.when(q < 4)
        def _():
            for link in BOTH:
                relay_copy(ten, q, link).start()

    def landed(ten, q):
        with jax.named_scope('landed'):
            wait(tile_part(ten, q, j), ld.at[ten, odd(q)])
            wait(tile_part(ten, q, other_core), f_recv.at[q, ten])

    def rows_of(r):
        return pl.ds(pl.multiple_of(r * tile, tile), tile)

    def load_a(ten, n):
        own = halved(n)
        slot = odd(n)

        @pl.when(own == 1)
        def _():
            pltpu.make_async_copy(tok[ten].at[rows_of(slot), :], tok_t[ten].at[slot], ld.at[ten, slot]).start()

        @pl.when(own == 0)
        def _():
            pltpu.make_async_copy(tok_p[ten].at[rows_of(slot), :], tok_t[ten].at[slot], ld.at[ten, slot]).start()

    def loaded(ten, slot):
        with jax.named_scope('ld'):
            wait(tok_t[ten].at[slot], ld.at[ten, slot])

    def unit_col(u):
        mine = cy * units
        other = (far_y) * units
        low = cx * rest_units
        high = (far_x) * near_units
        a = near_units
        col = jnp.where(u < a, mine + low + u,
                        jnp.where(u < units, mine + high + (u - a),
                                  jnp.where(u < units + a, other + low + (u - units), other + high + (u - units - a))))
        return pl.multiple_of(col * LANES, LANES)

    def chunk(s, way):
        n = lax.rem(s, steps)
        row = pl.multiple_of(way * tile + odd(n) * part_rows, part_rows)
        return lax.div(s, steps), pl.ds(row, part_rows), pl.ds(unit_col(halved(n)), LANES)

    def sum_copy(s, way, nxt):
        land = lax.rem(s, DEPTH)
        return send(yacc.at[chunk(s, way)], rbuf.at[way, land], rs_send.at[way, lax.rem(s, SLOTS)], rs_recv.at[way, land], tp=nxt)

    def done_copy(s, way, prv):
        ref = back.at[way, lax.rem(s, KEEP)]
        return send(ref, ref, ag_send.at[way, lax.rem(s, LAG + 1)], ag_recv.at[way, lax.rem(s, KEEP)], tp=prv)

    def store_copy(s, way):
        return pltpu.make_async_copy(back.at[way, lax.rem(s, KEEP)], yd_ref.at[chunk(s, way)],
                                     fin_own.at[way, lax.rem(s, LAG + 1)])

    def tick(tau):
        with jax.named_scope('tick'):
            tick_body(tau)

    def give(s, way, p, prv):
        @pl.when(s >= LAG)
        def _():
            store_copy(s - LAG, way).wait()

            @pl.when(p > 0)
            def _():
                wait(back.at[way, 0], ag_send.at[way, lax.rem(s - LAG, LAG + 1)])

        store_copy(s, way).start()

        @pl.when(p > 0)
        def _():
            done_copy(s, way, prv).start()

    def tick_body(tau):
        for way in BOTH:
            p = t if way == 0 else 3 - t
            nxt = t + 1 if way == 0 else t - 1
            prv = t - 1 if way == 0 else t + 1
            s = tau - HOP * p
            slot = lax.rem(jnp.maximum(s, 0), SLOTS)
            land = lax.rem(jnp.maximum(s, 0), DEPTH)
            live = jnp.logical_and(s >= 0, s < total)

            @pl.when(jnp.logical_and(live, p > 0))
            def _():
                wait(rbuf.at[way, land], rs_recv.at[way, land])

            @pl.when(jnp.logical_and(live, p < 3))
            def _():
                @pl.when(s >= SLOTS)
                def _():
                    wait(rbuf.at[way, 0], rs_send.at[way, slot])

                @pl.when(p > 0)
                def _():
                    here = chunk(s, way)
                    yacc[here] = yacc[here] + rbuf[way, land]

                sum_copy(s, way, nxt).start()

            @pl.when(jnp.logical_and(live, p == 3))
            def _():
                back[way, lax.rem(s, KEEP)] = (yacc[chunk(s, way)] + rbuf[way, land]).astype(BF16)
                give(s, way, p, prv)

        for way in BOTH:
            p = t if way == 0 else 3 - t
            prv = t - 1 if way == 0 else t + 1
            s = tau - HOP * (6 - p)

            @pl.when(jnp.logical_and(jnp.logical_and(s >= 0, s < total), p < 3))
            def _():
                keep = lax.rem(s, KEEP)
                wait(back.at[way, keep], ag_recv.at[way, keep])
                give(s, way, p, prv)

    def ticks(lo, hi):
        def body(n, c):
            tick(n)
            return c

        lax.fori_loop(lo, hi, body, 0)

    def drain_sums():
        for way in BOTH:
            p = t if way == 0 else 3 - t

            @pl.when(p < 3)
            def _():
                for slot in range(SLOTS):
                    wait(rbuf.at[way, 0], rs_send.at[way, slot])

            for m in range(LAG):
                s = total - LAG + m
                wait(back.at[way, 0], fin_own.at[way, s % (LAG + 1)])

                @pl.when(p > 0)
                def _():
                    wait(back.at[way, 0], ag_send.at[way, s % (LAG + 1)])

    w_start(0)
    w_start(1)
    for ten in BOTH:
        own_copy(ten).start()
    base = jnp.where(t == 0, 1.0, 0.0).astype(F32)

    with jax.named_scope('clear'):
        for r in BOTH:
            for ten in BOTH:
                load_a(ten, 2 + r)

        def clear(n, carry):
            at = pl.ds(pl.multiple_of(n * 32, 32), 32)
            acc_gu[at, :] = jnp.zeros((32, width), F32)
            acc_d[at, :] = jnp.zeros((32, half), F32)
            return carry

        lax.fori_loop(0, win // 32, clear, 0)

        def clear_ab(n, carry):
            lo = pl.ds(pl.multiple_of(n * group, group), group)
            for m in range(4):
                ab_all[m, lo, :] = jnp.zeros((group, width), F32)
            return carry

        lax.fori_loop(0, tile // group, clear_ab, 0)
        for r in BOTH:
            for ten in BOTH:
                loaded(ten, r)

                def residual(n, carry):
                    lo = pl.ds(pl.multiple_of(n * group, group), group)
                    there = pl.ds(pl.multiple_of(r * tile + n * group, group), group)
                    yacc[ten, there, :] = tok_t[ten][r, lo, :].astype(F32) * base
                    return carry

                lax.fori_loop(0, tile // group, residual, 0)
        for ten in BOTH:
            wait(tok_p[ten], own_recv.at[ten])

    with jax.named_scope('w_relay'):
        w_relay(0)
        w_relay(1)
    w_start(2)

    def side(n):
        return pl.ds(pl.multiple_of(odd(n) * half, LANES), half)

    def ab_pass(last):
        other = (far_y) * line
        if last:
            parts = ((other + (far_x) * near_units * LANES, rest_units * LANES),)
        else:
            parts = ((cy * line, line), (other + cx * rest_units * LANES, near_units * LANES))
        def body(n, carry):
            slot = odd(n)

            @pl.when(n < 3)
            def _():
                load_a(0, n + 1)

            loaded(0, slot)
            for at, size in parts:
                at_k = pl.ds(pl.multiple_of(at, LANES), size)
                with jax.named_scope('ab_part'):
                    for lo, hi in pieces:
                        ab_all[n, :, lo:hi] += dot_nn(xt[slot, :, at_k], w_gu[at_k, lo:hi])

            if last:
                def hidden(m, c):
                    lo = pl.ds(pl.multiple_of(m * group, group), group)
                    a = ab_all[n, lo, :half]
                    h_all[halved(n), lo, side(n)] = (a * sigmoid(a) * ab_all[n, lo, half:]).astype(BF16)
                    return c

                lax.fori_loop(0, tile // group, hidden, 0)
            return carry

        lax.fori_loop(0, 4, body, 0)

    load_a(0, 0)
    with jax.named_scope('w_have'):
        for k in BOTH:
            w_have(k, 'chip')
            w_have(k, 'x')
            w_have(k, 'y')
    ab_pass(0)
    load_a(0, 0)
    with jax.named_scope('w_have'):
        for k in BOTH:
            w_have(k, 'far')
    ab_pass(1)

    def y_group(g, tau):
        u0 = (0, near_units, units, units + near_units)[g]
        n_u = (near_units, rest_units)[g % 2]
        col = unit_col(u0)
        cols = pl.ds(col, n_u * LANES)

        def theirs(r, carry):
            if g > 0:
                before = (near_units, rest_units)[(g - 1) % 2] * LANES
                wait(sb.at[r, :, pl.ds(0, before)], y_send.at[(g - 1) % 2, r])
            with jax.named_scope('y_dot'):
                sb[r, :, :n_u * LANES] = dot_nt(h_all[0, :, side(r)], w_d[cols, :])
            send(sb.at[r, :, pl.ds(0, n_u * LANES)], pbuf.at[rows_of(r), cols],
                 y_send.at[g % 2, r], y_recv.at[g, r], dp=partner).start()
            return carry

        def ours(r, carry):
            with jax.named_scope('y_wait'):
                wait(pbuf.at[rows_of(r), cols], y_recv.at[g, r])
            with jax.named_scope('y_dot'):
                yacc[0, rows_of(r), cols] = (yacc[0, rows_of(r), cols] + pbuf[rows_of(r), cols]
                                             + dot_nt(h_all[1, :, side(r)], w_d[cols, :]))
            pl.semaphore_signal(credit, device_id={'dp': partner, 'tp': t}, device_id_type=MESH)
            return carry

        lax.fori_loop(0, 2, theirs, 0)
        if g > 0:
            tick(tau)
        lax.fori_loop(0, 2, ours, 0)
        if g > 0:
            tick(tau + 1)

    load_a(1, 0)
    load_a(0, 0)
    with jax.named_scope('w_have2'):
        w_have(2, 'chip')
    y_group(0, 0)
    tick(0)
    with jax.named_scope('w_relay2'):
        w_relay(2)
    q_start(0)
    q_start(1)
    ticks(1, 7)
    with jax.named_scope('w_have2'):
        w_have(2, 'x')
        w_have(2, 'y')
    y_group(1, 7)
    y_group(2, 9)
    q_start(2)
    ticks(11, 14)
    with jax.named_scope('w_have2'):
        w_have(2, 'far')
    y_group(3, 14)
    q_start(3)

    at_win, shift = window_of(chip * pair, win)
    own = own_window(blk)
    at_own, _ = window_of(me * blk, own)
    in_acc = pl.ds(pl.multiple_of(window_of(me * blk, own)[0].start - at_win.start, 8), own)
    n_block = len(ALL)
    n_cols = model // n_block

    def grad_copy(m):
        rows_ = pl.ds(pl.multiple_of(shift + (other_core) * blk, 8), blk)
        there = pl.ds(pl.multiple_of(window_of(partner * blk, own)[1], 8), blk)
        if m == 0:
            return send(acc_gu.at[rows_, :], pbuf.at[there, whole], out_send.at[0], out_recv.at[0], dp=partner)
        return send(acc_d.at[rows_, :], yacc.at[0, there, low], out_send.at[1], out_recv.at[1], dp=partner)

    def result_copy(ten):
        return pltpu.make_async_copy(yd_ref.at[ten], w_gu.at[pl.ds(ten * rows, rows), :], back_in.at[ten])

    def last_copy(m):
        if m != 1:
            middle = max(tile // group // 2, 1) * group
            at = pl.ds(0, middle) if m == 0 else pl.ds(middle, tile - middle)
            return send(h_all.at[1, at, :], xt.at[0, at, whole], h_send.at[m], h_recv.at[m], dp=partner)
        return send(h_all.at[0, :, low], dyt.at[0, :, low], h_send.at[1], h_recv.at[1], dp=partner)

    def dx_tile(n):
        r = odd(n)

        @pl.when(n == 0)
        def _():
            pl.semaphore_wait(credit, 8)
            for r_ in BOTH:
                wait(sb.at[r_, :, pl.ds(0, rest_units * LANES)], y_send.at[1, r_])

        def block(m, carry):
            cols = pl.ds(pl.multiple_of(m * n_cols, n_cols), n_cols)
            slot = lax.rem(m + r * n_block, 2)

            @pl.when(jnp.logical_and(n < 2, m + r * n_block >= 2))
            def _():
                wait(sb.at[slot], dx_send.at[slot])

            @pl.when(n < 2)
            def _():
                with jax.named_scope('dx_dot'):
                    sb[slot] = dot_nt(h_all[1], w_gu[cols, :])
                send(sb.at[slot], pbuf.at[rows_of(r), cols], dx_send.at[slot], dx_recv.at[r, m], dp=partner).start()

            @pl.when(n >= 2)
            def _():
                with jax.named_scope('dx_wait'):
                    wait(pbuf.at[rows_of(r), cols], dx_recv.at[r, m])
                with jax.named_scope('dx_dot'):
                    yacc[1, rows_of(r), cols] = (yacc[1, rows_of(r), cols] + pbuf[rows_of(r), cols]
                                                 + dot_nt(h_all[1], w_gu[cols, :]))

            @pl.when(m >= 1)
            def _():
                tick(17 + 4 * n + m)
            return carry

        lax.fori_loop(0, n_block, block, 0)

    def grad_tile(n, carry):
        q = n - 4
        home = n < 4
        token = n >= 4
        slot = odd(n)
        at = jnp.where(home, n, slot)
        final = n == 15
        early = jnp.logical_and(n >= 3, q + 1 <= EARLY)
        late = jnp.logical_and(n < 15, q + 1 > EARLY)
        dense = q >= 8
        extra = jnp.logical_and(dense, q < 10)
        tau = jnp.where(dense, 64 + 5 * (q - 8), 16 + 4 * n)
        late_step = jnp.where(final, 1, 0)

        @pl.when(home)
        def _():
            q_start(4 + n)
            loaded(0, slot)

        @pl.when(extra)
        def _():
            tick(tau)

        step = jnp.where(extra, tau + 1, tau)

        @pl.when(token)
        def _():
            landed(0, q)
            with jax.named_scope('ab_dot'):
                ab_all[at, :, :cut_ab] = dot_nn(xt[slot], w_gu[:, :cut_ab])
            tick(step)

            @pl.when(jnp.logical_and(q > MIDDLE, n < 15))
            def _():
                arrive(1, q)

            with jax.named_scope('ab_dot'):
                ab_all[at, :, cut_ab:] = dot_nn(xt[slot], w_gu[:, cut_ab:])

            @pl.when(final)
            def _():
                pl.semaphore_wait(room.at[1], 2)
                arrive(1, q)
                tick(tau + 1)
                with jax.named_scope('h_last'):
                    def body(m, c):
                        lo = pl.ds(pl.multiple_of(m * group, group), group)
                        a = ab_all[at, lo, :half]
                        h_all[0, lo, :half] = (a * sigmoid(a) * ab_all[at, lo, half:]).astype(BF16)
                        return c

                    lax.fori_loop(0, tile // group, body, 0)
                    last_copy(1).start()
                    grad_copy(1).start()
                    w_relayed((0, 1))
                    result_copy(0).start()

        @pl.when(early)
        def _():
            arrive(0, q + 1)
            arrive(1, q + 1)

        @pl.when(home)
        def _():
            loaded(1, slot)

        @pl.when(token)
        def _():
            landed(1, q)

        with jax.named_scope('g_dot'):
            g_s[:, :cut_g] = dot_nn(dyt[slot], w_d[:, :cut_g])

        @pl.when(token)
        def _():
            tick(step + 1 + late_step)

        with jax.named_scope('g_dot'):
            g_s[:, cut_g:] = dot_nn(dyt[slot], w_d[:, cut_g:])

        def activate(with_h, start=0, stop=tile // group):
            def body(m, c):
                lo = pl.ds(pl.multiple_of(m * group, group), group)
                a = ab_all[at, lo, :half]
                b = ab_all[at, lo, half:]
                g = g_s[lo, :]
                s = sigmoid(a)
                silu = a * s
                if with_h:
                    h_all[0, lo, :half] = (silu * b).astype(BF16)
                h_all[1, lo, :half] = (g * b * s * (ONE + a * (ONE - s))).astype(BF16)
                h_all[1, lo, half:] = (g * silu).astype(BF16)
                return c

            with jax.named_scope('act'):
                lax.fori_loop(start, stop, body, 0)

        @pl.when(final)
        def _():
            middle = max(tile // group // 2, 1)
            activate(False, 0, middle)
            pl.semaphore_wait(room.at[0])
            last_copy(0).start()
            activate(False, middle)
            last_copy(2).start()

        @pl.when(jnp.logical_not(final))
        def _():
            activate(True)

        tick(step + jnp.where(home, 0, 2 + late_step))

        @pl.when(n < 3)
        def _():
            load_a(0, n + 1)
            load_a(1, n + 1)

        @pl.when(late)
        def _():
            arrive(0, q + 1)

        @pl.when(n == 14)
        def _():
            tick(tau + 3)

        @pl.when(jnp.logical_not(final))
        def _():
            with jax.named_scope('dw_dot'):
                for lo in range(0, width, third):
                    hi = lo + third
                    acc_gu[:, lo:hi] += dot_tn(xt[slot, :, at_win], h_all[1, :, lo:hi])

            @pl.when(n == 14)
            def _():
                grad_copy(0).start()

            with jax.named_scope('dw_dot2'):
                for lo, hi in ((0, half_cut), (half_cut, half)):
                    acc_d[:, lo:hi] += dot_tn(dyt[slot, :, at_win], h_all[0, :, lo:hi])

        @pl.when(final)
        def _():
            with jax.named_scope('grads_sent'):
                grad_copy(0).wait_send()
            with jax.named_scope('dw_own'):
                for lo, hi in pieces:
                    acc_gu[in_acc, lo:hi] += dot_tn(xt[1, :, at_own], h_all[1, :, lo:hi])
            with jax.named_scope('grads_sent'):
                grad_copy(1).wait_send()
            with jax.named_scope('dw_own'):
                acc_d[in_acc, :] += dot_tn(dyt[1, :, at_own], h_all[0, :, :half])

        @pl.when(jnp.logical_and(n >= 2, n < 15))
        def _():
            for ten in BOTH:
                pl.semaphore_signal(room.at[ten], device_id={'dp': partner, 'tp': t}, device_id_type=MESH)

        tick(step + jnp.where(home, 1, jnp.where(n < 14, 3, 4)))

        @pl.when(home)
        def _():
            dx_tile(n)

        @pl.when(jnp.logical_and(late, q + 1 <= MIDDLE))
        def _():
            arrive(1, q + 1)
        return carry

    lax.fori_loop(0, 16, grad_tile, 0)

    theirs = pl.ds(pl.multiple_of(window_of(me * blk, own)[1], 8), blk)
    with jax.named_scope('last_wait_h'):
        wait(yacc.at[0, theirs, low], out_recv.at[1])
        wait(dyt.at[0, :, low], h_recv.at[1])
    with jax.named_scope('dw_other'):
        yacc[0, :own, :half] += dot_tn(dyt[1, :, at_own], dyt[0, :, :half])
    with jax.named_scope('drain_sums'):
        drain_sums()
    result_copy(1).start()
    with jax.named_scope('last_wait'):
        wait(pbuf.at[theirs, whole], out_recv.at[0])
        for m in (0, 2):
            last_copy(m).wait_recv()
    with jax.named_scope('dw_other'):
        for lo, hi in pieces:
            pbuf[:own, lo:hi] += dot_tn(xt[1, :, at_own], xt[0, :, lo:hi])

    with jax.named_scope('drain'):
        for ten in BOTH:
            result_copy(ten).wait()
        for slot in BOTH:
            wait(sb.at[slot], dx_send.at[slot])
        for k in ALL:
            for core in BOTH:
                for link in BOTH:
                    for part in BOTH:
                        w_copy(k, link, part, core).wait_send()
            w_partner_copy(k).wait_send()
        w_relayed((2,))
        for ten in BOTH:
            own_copy(ten).wait_send()

        def drain(q, carry):
            for ten in BOTH:
                wait(tok_b[ten].at[0], f_send.at[q, ten])
                for link in BOTH:
                    @pl.when(q < 8)
                    def _():
                        wait(slot_of(ten, 0, link), q_send.at[lax.rem(q, 8), link, ten])

                    @pl.when(q < 4)
                    def _():
                        wait(slot_of(ten, 0, link), rl_send.at[lax.rem(q, 4), link, ten])

            return carry

        lax.fori_loop(0, 12, drain, 0)
        for m in ALL:
            last_copy(m).wait_send()


def window_of(start, size):
    first = lax.div(start, LANES) * LANES
    return pl.ds(pl.multiple_of(first, LANES), size), start - first


def own_window(blk):
    return -(-(blk + LANES - 32) // LANES) * LANES


def window(model, blk):
    starts = [(2 * blk * c) // LANES * LANES for c in range(model // (2 * blk))]
    shift = max(2 * blk * c - s for c, s in enumerate(starts))
    return -(-(shift + 2 * blk) // LANES) * LANES


def mlp(x, dy, wg, wu, wd):
    rows, model = x.shape
    blk, width = wg.shape
    half = width // 2
    tile = rows // 2
    dma = pltpu.SemaphoreType.DMA
    two, three, four = dma((2,)), dma((3,)), dma((2, 2))
    six, many, pieces_ = dma((3, 2, 2)), dma((12, 2)), dma((3, 2, 2, 2))
    vmem = pltpu.VMEM
    anywhere = pl.BlockSpec(memory_space=pl.ANY)
    shape = jax.ShapeDtypeStruct
    flops = 2 * model * half * rows * 2 * 20
    win = window(model, blk)
    most = max(rows, own_window(blk))
    kept = (vmem((win, 2 * half), F32), vmem((win, half), F32), vmem((most, model), F32), vmem((2, most, model), F32))
    kept = (*kept, vmem((model, 2 * half), BF16))
    held = sum(k.dtype.itemsize * math.prod(k.shape) for k in kept)
    in_vmem = pl.BlockSpec(memory_space=pltpu.VMEM)
    return pl.pallas_call(
        kernel,
        name='mlp',
        out_shape=(shape((2, rows, model), BF16), *kept,
                   shape((12, tile // 2, model), BF16), shape((12, tile // 2, model), BF16),
                   shape((rows, model), BF16), shape((rows, model), BF16)),
        in_specs=[anywhere] * 5,
        out_specs=(anywhere, *[in_vmem] * 5, *[anywhere] * 4),
        scratch_shapes=[
            vmem((model, half), BF16),
            vmem((2, tile, model // 3), F32),
            vmem((2, tile, model), BF16),
            vmem((2, tile, model), BF16),
            vmem((4, tile, 2 * half), F32),
            vmem((tile, half), F32),
            vmem((2, tile, 2 * half), BF16),
            vmem((2, DEPTH, tile // 2, LANES), F32),
            vmem((2, KEEP, tile // 2, LANES), BF16),
            pieces_, pieces_, six, six, three, three, three,
            two, two, dma((8, 2, 2)), dma((12, 2, 2)), dma((4, 2, 2)), many, many,
            four, dma((4, 2)), two, dma((2, 3)), pltpu.SemaphoreType.REGULAR, pltpu.SemaphoreType.REGULAR((2,)),
            dma((2, SLOTS)), dma((2, DEPTH)), dma((2, LAG + 1)), dma((2, KEEP)), dma((2, LAG + 1)),
            four, two, two, three, three, two,
        ],
        compiler_params=pltpu.CompilerParams(collective_id=0, has_side_effects=True, vmem_limit_bytes=67_000_000 - held),
        cost_estimate=pl.CostEstimate(flops=flops, bytes_accessed=100_000_000, transcendentals=0),
    )(x, dy, wg, wu, wd)


def results_kernel(blk, half, acc_gu, acc_d, pbuf, yacc, w_gu, y_out, dx_out, g_out, u_out, d_out, sem):
    me = lax.axis_index('dp')
    j = odd(me)
    chip = halved(me)
    rows = y_out.shape[0]
    mine = pl.ds(pl.multiple_of(window_of(chip * 2 * blk, LANES)[1] + j * blk, 8), blk)
    other = pl.ds(pl.multiple_of(window_of(me * blk, LANES)[1], 8), blk)
    own_cols = pl.ds(pl.multiple_of(j * half, LANES), half)
    other_cols = pl.ds(pl.multiple_of((1 - j) * half, LANES), half)
    low, high = pl.ds(0, half), pl.ds(half, half)
    copies = [pltpu.make_async_copy(src, dst, sem.at[n]) for n, (src, dst) in enumerate((
        (acc_gu.at[mine, low], g_out.at[:, own_cols]), (acc_gu.at[mine, high], u_out.at[:, own_cols]),
        (acc_d.at[mine, :], d_out.at[:, own_cols]),
        (pbuf.at[other, low], g_out.at[:, other_cols]), (pbuf.at[other, high], u_out.at[:, other_cols]),
        (yacc.at[0, other, low], d_out.at[:, other_cols]),
        (w_gu.at[pl.ds(0, rows), :], y_out), (w_gu.at[pl.ds(rows, rows), :], dx_out)))]
    for copy in copies:
        copy.start()
    for copy in copies:
        copy.wait()


def results(blk, width, rows, *kept):
    anywhere = pl.BlockSpec(memory_space=pl.ANY)
    in_vmem = pl.BlockSpec(memory_space=pltpu.VMEM)
    shape = jax.ShapeDtypeStruct
    model = kept[-1].shape[0]
    kept = [pltpu.with_memory_space_constraint(k, pltpu.VMEM) for k in kept]
    return pl.pallas_call(
        functools.partial(results_kernel, blk, width // 2),
        name='results',
        out_shape=(shape((rows, model), BF16), shape((rows, model), BF16),
                   shape((blk, width), F32), shape((blk, width), F32), shape((blk, width), F32)),
        in_specs=[in_vmem] * 5,
        out_specs=tuple([anywhere] * 5),
        scratch_shapes=[pltpu.SemaphoreType.DMA((8,))],
        compiler_params=pltpu.CompilerParams(vmem_limit_bytes=4_000_000),
    )(*kept)


def solution(mesh):
    def device_pass(x_rows, gate_blk, up_blk, down_blk, dy_rows):
        out = mlp(x_rows, dy_rows, gate_blk, up_blk, down_blk.T)
        y, dx, dw_gate, dw_up, dw_down = results(*gate_blk.shape, x_rows.shape[0], *out[1:6])
        return y, dx, dw_gate, dw_up, dw_down.T

    row_spec = P('dp', None)
    weight_spec = P('dp', 'tp')
    down_spec = P('tp', 'dp')
    return jax.shard_map(device_pass, mesh=mesh,
                         in_specs=(row_spec, weight_spec, weight_spec, down_spec, row_spec),
                         out_specs=(row_spec, row_spec, weight_spec, weight_spec, down_spec),
                         check_vma=False)
```

profile of v0, /device:TPU:0, one launch (start us, length us, event | category | flops | bytes accessed | tf_op | source)
XLA Modules:
  0.0 303.0 jit_solution(12150003101780740391)
XLA Ops:
  0.6 297.5 %mlp.1 = (bf16[2,512,2304]{2,1,0:T(8,128)(2,1)}, f32[640,2304]{1,0:T(8,128)S(1)}, f32[640,1152]{1,0:T(8,128)S(1)}, f32[512,2304]{1,0:T(8,128)S(1)}, f32[2,512,23...) custom-call(bf16[512,2304]{1,0:T(8,128)(2,1)} %x_ref.1, ...), custom_call_target="tpu_custom_call" | custom-call | flops 108716359680 | bytes 100000000 | tf_op jit(solution)/shard_map/mlp/pallas_call | solution.py:840
  298.1 4.7 %results.1 = (bf16[512,2304]{1,0:T(8,128)(2,1)}, bf16[512,2304]{1,0:T(8,128)(2,1)}, f32[288,2304]{1,0:T(8,128)}, f32[288,2304]{1,0:T(8,128)}, f32[288,2304]{1,0:T(8,128)}) custom-call(f32[640,2304]{1,0:T(8,128)S(1)} %get-tuple-element.15.acc_gu, f32[640,1152]{1,0:T(8,128)S(1)} %get-tuple-element.16.acc_d, f32[512,2304]{1,0:T(8,128)S(1)} %get-tuple-element.17.pbuf, ...), custom_call_target="tpu_custom_call" | custom-call | tf_op jit(solution)/shard_map/results/pallas_call | solution.py:897
where the time goes:
time: 303 us
  Pallas kernels  302 us (100%)
    pallas_call x1, Pallas kernels, mlp(): pl.pallas_call(kernel, name='mlp', out_shape=(shape((2, rows, model), BF1...  297 us

commit v1 on v0

--- a/solution.py
+++ b/solution.py
@@ -595,7 +595,8 @@
         dense = q >= 8
         extra = jnp.logical_and(dense, q < 10)
         tau = jnp.where(dense, 64 + 5 * (q - 8), 16 + 4 * n)
-        late_step = jnp.where(final, 1, 0)
+        tau = jnp.where(final, 78, tau)
+        late_step = jnp.where(final, 2, 0)
 
         @pl.when(home)
         def _():
@@ -637,7 +638,8 @@
                     lax.fori_loop(0, tile // group, body, 0)
                     last_copy(1).start()
                     grad_copy(1).start()
-                    w_relayed((0, 1))
+                    tick(tau + 2)
+                    w_relayed(BOTH)
                     result_copy(0).start()
 
         @pl.when(early)
@@ -704,10 +706,6 @@
         def _():
             arrive(0, q + 1)
 
-        @pl.when(n == 14)
-        def _():
-            tick(tau + 3)
-
         @pl.when(jnp.logical_not(final))
         def _():
             with jax.named_scope('dw_dot'):
@@ -718,6 +716,7 @@
             @pl.when(n == 14)
             def _():
                 grad_copy(0).start()
+                tick(tau + 3)
 
             with jax.named_scope('dw_dot2'):
                 for lo, hi in ((0, half_cut), (half_cut, half)):
@@ -740,7 +739,7 @@
             for ten in BOTH:
                 pl.semaphore_signal(room.at[ten], device_id={'dp': partner, 'tp': t}, device_id_type=MESH)
 
-        tick(step + jnp.where(home, 1, jnp.where(n < 14, 3, 4)))
+        tick(step + jnp.where(home, 1, jnp.where(n < 14, 3, jnp.where(final, 5, -100))))
 
         @pl.when(home)
         def _():

time: 303 us -> 304 us (level)
  no operation moved by 1% of the time
where the time goes in v1:
time: 304 us
  Pallas kernels  303 us (100%)
    pallas_call x1, Pallas kernels, mlp(): pl.pallas_call(kernel, name='mlp', out_shape=(shape((2, rows, model), BF1...  298 us

profile of v1, /device:TPU:0, one launch (start us, length us, event | category | flops | bytes accessed | tf_op | source)
XLA Modules:
  0.0 303.6 jit_solution(5593311453396921466)
XLA Ops:
  0.6 298.0 %mlp.1 = (bf16[2,512,2304]{2,1,0:T(8,128)(2,1)}, f32[640,2304]{1,0:T(8,128)S(1)}, f32[640,1152]{1,0:T(8,128)S(1)}, f32[512,2304]{1,0:T(8,128)S(1)}, f32[2,512,23...) custom-call(bf16[512,2304]{1,0:T(8,128)(2,1)} %x_ref.1, ...), custom_call_target="tpu_custom_call" | custom-call | flops 108716359680 | bytes 100000000 | tf_op jit(solution)/shard_map/mlp/pallas_call | solution.py:839
  298.7 4.7 %results.1 = (bf16[512,2304]{1,0:T(8,128)(2,1)}, bf16[512,2304]{1,0:T(8,128)(2,1)}, f32[288,2304]{1,0:T(8,128)}, f32[288,2304]{1,0:T(8,128)}, f32[288,2304]{1,0:T(8,128)}) custom-call(f32[640,2304]{1,0:T(8,128)S(1)} %get-tuple-element.15.acc_gu, f32[640,1152]{1,0:T(8,128)S(1)} %get-tuple-element.16.acc_d, f32[512,2304]{1,0:T(8,128)S(1)} %get-tuple-element.17.pbuf, ...), custom_call_target="tpu_custom_call" | custom-call | tf_op jit(solution)/shard_map/results/pallas_call | solution.py:896
